TPU v7x, 32 devices: a whole 2x2x4 slice. The times are simulated.
32 devices in a mesh: row: 4 (over z), col: 8 (over y, x, core).
Axes of the slice: x: 2, y: 2, z: 4, core: 2. Of those that a mesh axis runs over, the one named last changes fastest.
Arguments:
- rhs: float32 [64, 131072], P(None, ('row', 'col')), may hold values from -6 to 6
- pivots: int32 [4096], replicated, may hold values from 0 to 131071, as said below
- factor: float32 [4096, 4, 8, 128], P('row', None, 'col'), as said below
- diag_inv: float32 [8, 512, 512], P('row'), as said below
Outputs:
- solution: float32 [64, 4, 8, 128], P(None, None, 'col')
Inputs may be any that keep to these rules, and one draw needn't show every extreme that they name: `pivots`: distinct column numbers, the first 4096 entries of a permutation of 0 .. 131071. `factor`: entry (row i, column q) is zero where q >= 512 * (i // 512). `diag_inv`: each block is unit lower triangular.
All inputs are finite; a program needn't handle non-finite values.
Results may differ from a plain program's by a relative error of at most 0.0001.
Values sent between devices are 32-bit elements; how exact they have to be, the bound alone decides.
A program may use at most 64 MiB of HBM per device.

v0:
```python
import jax
import jax.numpy as jnp
from jax import lax
from jax.sharding import PartitionSpec as P


def broadcast(shard, axis, root):
    mine = lax.axis_index(axis) == root
    return lax.psum(jnp.where(mine, shard, jnp.zeros_like(shard)), axis)


def apply_inverse(values, block_inv):
    return lax.dot_general(
        values,
        block_inv,
        (((1,), (1,)), ((), ())),
        precision=lax.Precision.HIGHEST,
        preferred_element_type=jnp.float32,
    )


def per_device(rhs, pivots, factor, diag_inv):
    my_row = lax.axis_index("row")
    my_col = lax.axis_index("col")
    col_count = lax.axis_size("col")
    rhs_count = rhs.shape[0]
    slab_rows = factor.shape[0]
    rounds = factor.shape[1]
    piece_len = factor.shape[3]
    block_len = diag_inv.shape[1]
    pieces = block_len // piece_len
    blocks_here = slab_rows // block_len
    total_blocks = blocks_here * lax.axis_size("row")
    first_column = (my_row * col_count + my_col) * rhs.shape[1]
    source_len = rhs.shape[1]
    located = pivots - first_column
    inside = (located >= 0) & (located < source_len)
    taken = jnp.take(rhs, jnp.clip(located, 0, source_len - 1), axis=1)
    taken = jnp.where(inside[None, :], taken, 0.0)
    permuted = lax.psum_scatter(
        jnp.transpose(
            taken.reshape(rhs_count, blocks_here * lax.axis_size("row"), block_len), (1, 0, 2)
        ),
        "row",
        scatter_dimension=0,
        tiled=True,
    )
    permuted = lax.psum(permuted, "col")
    factor_rows = factor.reshape(slab_rows, rounds * piece_len)

    def advance(number, solved):
        owner_row = number // blocks_here
        local_block = number % blocks_here
        block_rows = lax.dynamic_slice_in_dim(factor_rows, local_block * block_len, block_len, 0)
        partial_value = lax.dot_general(
            solved.reshape(rhs_count, rounds * piece_len),
            block_rows,
            (((1,), (1,)), ((), ())),
            precision=lax.Precision.HIGHEST,
            preferred_element_type=jnp.float32,
        )
        own_rhs = lax.dynamic_index_in_dim(permuted, local_block, 0, keepdims=False)
        block_inv = lax.dynamic_index_in_dim(diag_inv, local_block, 0, keepdims=False)
        summed = lax.psum(partial_value, "col")
        fresh = apply_inverse(own_rhs - summed, block_inv)
        fresh = broadcast(fresh, "row", owner_row)
        first_piece = number * pieces
        offset_piece = (my_col - first_piece) % col_count
        owns = offset_piece < pieces
        which = jnp.clip(offset_piece, 0, pieces - 1)
        local_round = jnp.clip((first_piece + offset_piece) // col_count, 0, rounds - 1)
        piece = lax.dynamic_slice_in_dim(fresh, which * piece_len, piece_len, 1)
        updated = lax.dynamic_update_index_in_dim(solved, piece[:, None, :], local_round, 1)
        return jnp.where(owns, updated, solved)

    start_state = jnp.zeros((rhs_count, rounds, 1, piece_len), jnp.float32)
    return lax.fori_loop(0, total_blocks, advance, start_state)


def solution(mesh):
    return jax.shard_map(
        per_device,
        mesh=mesh,
        in_specs=(P(None, ("row", "col")), P(), P("row", None, "col", None), P("row", None, None)),
        out_specs=P(None, None, "col", None),
        check_vma=False,
    )
```

profile of v0, /device:TPU:0, one launch (start us, length us, event | category | flops | bytes accessed | tf_op | source)
XLA Modules:
  0.0 882.2 jit_solution(17491685887215917001)
XLA Ops:
  6.5 0.7 compare_and_fusion.1
  7.3 0.7 fusion.8
  8.1 1.8 copy.8
  9.9 14.1 %gather_fusion = f32[4096,64]{1,0:T(8,128)} fusion(f32[64,4096]{0,1:T(8,128)S(1)} %copy.8, s32[4096]{0:T(1024)S(1)} %fusion.8), kind=kCustom, calls=%fused_computation | custom fusion | bytes 2113536 | tf_op jit(solution)/shard_map/jit(_take)/gather | solution.py:38
  24.0 2.2 copy.9
  26.2 1.2 select_bitcast_fusion
  27.4 30.1 %reduce-scatter.2.cloned.1.call-done = f32[2,64,512]{2,1,0:T(8,128)} async-done(((f32[8,64,512]{2,1,0:T(8,128)}), f32[2,64,512]{2,1,0:T(8,128)}) %reduce-scatter.2.cloned.1.call-update) | async-done | bytes 262160 | tf_op jit(solution)/shard_map/reduce_scatter | solution.py:40
  57.5 1.8 copy.18
  59.3 53.7 %all-reduce.4.cloned.1.call-done = f32[2,64,512]{2,1,0:T(8,128)} async-done(((f32[2,64,512]{2,1,0:T(8,128)}), f32[2,64,512]{2,1,0:T(8,128)}) %all-reduce.4.cloned.1.call-update) | async-done | bytes 262160 | tf_op jit(solution)/shard_map/psum | solution.py:48
  113.0 761.7 %while.16 = (s32[]{:T(128)}, f32[64,4,1,128]{3,1,0,2:T(4,128)S(1)}, s32[]{:T(128)}, f32[2,64,512]{2,1,0:T(8,128)}, f32[1024,512]{1,0:T(8,128)S(1)}, /*index=5*/f...) while((s32[]{:T(128)}, f32[64,4,1,128]{3,1,0,2:T(4,128)S(1)}, ...), condition=%wide.region_5.6_spmd, body=%wide.region_2.5_spmd.sunk | while | flops 402792448 | bytes 4557184 | solution.py:77
  113.1 1.8 convolution_bitcast_fusion.2
  114.9 0.0 all-reduce.8.cloned.1.call-start
  115.0 54.8 %all-reduce.6.cloned.1.call-done = f32[64,512]{1,0:T(8,128)} async-done(((f32[64,512]{1,0:T(8,128)}), f32[64,512]{1,0:T(8,128)}) %all-reduce.6.cloned.1.call-update) | async-done | bytes 131088 | tf_op jit(solution)/shard_map/while/body/eval_jaxpr/psum | solution.py:64
  169.7 3.1 convolution_select_fusion.2
  172.9 34.1 %all-reduce.8.cloned.1.call-done = f32[64,512]{1,0:T(8,128)} async-done(((f32[64,512]{1,0:T(8,128)}), f32[64,512]{1,0:T(8,128)}) %all-reduce.8.cloned.1.call-update) | async-done | bytes 131088 | tf_op jit(solution)/shard_map/while/body/eval_jaxpr/psum | solution.py:9
  207.1 0.8 constant_dynamic-slice_fusion.2
  207.9 0.2 select_n.202
  208.1 1.8 convolution_bitcast_fusion.2
  209.9 0.0 all-reduce.8.cloned.1.call-start
  210.0 54.8 %all-reduce.6.cloned.1.call-done = f32[64,512]{1,0:T(8,128)} async-done(((f32[64,512]{1,0:T(8,128)}), f32[64,512]{1,0:T(8,128)}) %all-reduce.6.cloned.1.call-update) | async-done | bytes 131088 | tf_op jit(solution)/shard_map/while/body/eval_jaxpr/psum | solution.py:64
  264.8 3.1 convolution_select_fusion.2
  268.0 34.1 %all-reduce.8.cloned.1.call-done = f32[64,512]{1,0:T(8,128)} async-done(((f32[64,512]{1,0:T(8,128)}), f32[64,512]{1,0:T(8,128)}) %all-reduce.8.cloned.1.call-update) | async-done | bytes 131088 | tf_op jit(solution)/shard_map/while/body/eval_jaxpr/psum | solution.py:9
  302.1 0.8 constant_dynamic-slice_fusion.2
  302.9 0.2 select_n.202
  303.2 1.8 convolution_bitcast_fusion.2
  305.0 0.0 all-reduce.8.cloned.1.call-start
  305.1 55.1 %all-reduce.6.cloned.1.call-done = f32[64,512]{1,0:T(8,128)} async-done(((f32[64,512]{1,0:T(8,128)}), f32[64,512]{1,0:T(8,128)}) %all-reduce.6.cloned.1.call-update) | async-done | bytes 131088 | tf_op jit(solution)/shard_map/while/body/eval_jaxpr/psum | solution.py:64
  360.1 3.1 convolution_select_fusion.2
  363.3 34.1 %all-reduce.8.cloned.1.call-done = f32[64,512]{1,0:T(8,128)} async-done(((f32[64,512]{1,0:T(8,128)}), f32[64,512]{1,0:T(8,128)}) %all-reduce.8.cloned.1.call-update) | async-done | bytes 131088 | tf_op jit(solution)/shard_map/while/body/eval_jaxpr/psum | solution.py:9
  397.5 0.8 constant_dynamic-slice_fusion.2
  398.3 0.2 select_n.202
  398.5 1.8 convolution_bitcast_fusion.2
  400.4 0.0 all-reduce.8.cloned.1.call-start
  400.4 55.1 %all-reduce.6.cloned.1.call-done = f32[64,512]{1,0:T(8,128)} async-done(((f32[64,512]{1,0:T(8,128)}), f32[64,512]{1,0:T(8,128)}) %all-reduce.6.cloned.1.call-update) | async-done | bytes 131088 | tf_op jit(solution)/shard_map/while/body/eval_jaxpr/psum | solution.py:64
  455.5 3.1 convolution_select_fusion.2
  458.7 34.1 %all-reduce.8.cloned.1.call-done = f32[64,512]{1,0:T(8,128)} async-done(((f32[64,512]{1,0:T(8,128)}), f32[64,512]{1,0:T(8,128)}) %all-reduce.8.cloned.1.call-update) | async-done | bytes 131088 | tf_op jit(solution)/shard_map/while/body/eval_jaxpr/psum | solution.py:9
  492.8 0.8 constant_dynamic-slice_fusion.2
  493.6 0.2 select_n.202
  493.9 1.8 convolution_bitcast_fusion.2
  495.7 0.0 all-reduce.8.cloned.1.call-start
  495.8 55.1 %all-reduce.6.cloned.1.call-done = f32[64,512]{1,0:T(8,128)} async-done(((f32[64,512]{1,0:T(8,128)}), f32[64,512]{1,0:T(8,128)}) %all-reduce.6.cloned.1.call-update) | async-done | bytes 131088 | tf_op jit(solution)/shard_map/while/body/eval_jaxpr/psum | solution.py:64
  550.9 3.1 convolution_select_fusion.2
  554.1 34.1 %all-reduce.8.cloned.1.call-done = f32[64,512]{1,0:T(8,128)} async-done(((f32[64,512]{1,0:T(8,128)}), f32[64,512]{1,0:T(8,128)}) %all-reduce.8.cloned.1.call-update) | async-done | bytes 131088 | tf_op jit(solution)/shard_map/while/body/eval_jaxpr/psum | solution.py:9
  588.2 0.8 constant_dynamic-slice_fusion.2
  589.0 0.2 select_n.202
  589.3 1.8 convolution_bitcast_fusion.2
  591.1 55.1 %all-reduce.6.cloned.1.call-done = f32[64,512]{1,0:T(8,128)} async-done(((f32[64,512]{1,0:T(8,128)}), f32[64,512]{1,0:T(8,128)}) %all-reduce.6.cloned.1.call-update) | async-done | bytes 131088 | tf_op jit(solution)/shard_map/while/body/eval_jaxpr/psum | solution.py:64
  646.2 3.1 convolution_select_fusion.2
  649.4 34.1 %all-reduce.8.cloned.1.call-done = f32[64,512]{1,0:T(8,128)} async-done(((f32[64,512]{1,0:T(8,128)}), f32[64,512]{1,0:T(8,128)}) %all-reduce.8.cloned.1.call-update) | async-done | bytes 131088 | tf_op jit(solution)/shard_map/while/body/eval_jaxpr/psum | solution.py:9
  683.6 0.8 constant_dynamic-slice_fusion.2
  684.4 0.2 select_n.202
  684.6 1.8 convolution_bitcast_fusion.2
  686.5 54.8 %all-reduce.6.cloned.1.call-done = f32[64,512]{1,0:T(8,128)} async-done(((f32[64,512]{1,0:T(8,128)}), f32[64,512]{1,0:T(8,128)}) %all-reduce.6.cloned.1.call-update) | async-done | bytes 131088 | tf_op jit(solution)/shard_map/while/body/eval_jaxpr/psum | solution.py:64
  741.3 3.1 convolution_select_fusion.2
  744.5 34.1 %all-reduce.8.cloned.1.call-done = f32[64,512]{1,0:T(8,128)} async-done(((f32[64,512]{1,0:T(8,128)}), f32[64,512]{1,0:T(8,128)}) %all-reduce.8.cloned.1.call-update) | async-done | bytes 131088 | tf_op jit(solution)/shard_map/while/body/eval_jaxpr/psum | solution.py:9
  778.6 0.8 constant_dynamic-slice_fusion.2
  779.4 0.2 select_n.202
  779.7 1.8 convolution_bitcast_fusion.2
  781.6 54.8 %all-reduce.6.cloned.1.call-done = f32[64,512]{1,0:T(8,128)} async-done(((f32[64,512]{1,0:T(8,128)}), f32[64,512]{1,0:T(8,128)}) %all-reduce.6.cloned.1.call-update) | async-done | bytes 131088 | tf_op jit(solution)/shard_map/while/body/eval_jaxpr/psum | solution.py:64
  836.3 3.1 convolution_select_fusion.2
  839.5 34.1 %all-reduce.8.cloned.1.call-done = f32[64,512]{1,0:T(8,128)} async-done(((f32[64,512]{1,0:T(8,128)}), f32[64,512]{1,0:T(8,128)}) %all-reduce.8.cloned.1.call-update) | async-done | bytes 131088 | tf_op jit(solution)/shard_map/while/body/eval_jaxpr/psum | solution.py:9
  873.7 0.8 constant_dynamic-slice_fusion.2
  874.5 0.2 select_n.202
  874.7 0.6 copy-done
  (43 shorter events, 1.2 us)
Async XLA Ops:
  6.5 51.0 %reduce-scatter.2.cloned.1.call-start = ((), (), s32[]{:S(2)}) async-start(), calls=%async_computation.1 | async-start | bytes 1310720 | tf_op jit(solution)/shard_map/reduce_scatter | solution.py:40
  27.3 85.6 %all-reduce.4.cloned.1.call-start = ((), (), s32[]{:S(2)}) async-start(), calls=%async_computation.2 | async-start | bytes 524288 | tf_op jit(solution)/shard_map/psum | solution.py:48
  113.0 56.7 %all-reduce.6.cloned.1.call-start = ((), (), s32[]{:S(2)}) async-start(), calls=%async_computation.3 | async-start | bytes 262144 | tf_op jit(solution)/shard_map/while/body/eval_jaxpr/psum | solution.py:64
  114.9 92.2 %all-reduce.8.cloned.1.call-start = ((), (), s32[]{:S(2)}) async-start(), calls=%async_computation.4 | async-start | bytes 262144 | tf_op jit(solution)/shard_map/while/body/eval_jaxpr/psum | solution.py:9
  208.1 56.7 %all-reduce.6.cloned.1.call-start = ((), (), s32[]{:S(2)}) async-start(), calls=%async_computation.3 | async-start | bytes 262144 | tf_op jit(solution)/shard_map/while/body/eval_jaxpr/psum | solution.py:64
  209.9 92.2 %all-reduce.8.cloned.1.call-start = ((), (), s32[]{:S(2)}) async-start(), calls=%async_computation.4 | async-start | bytes 262144 | tf_op jit(solution)/shard_map/while/body/eval_jaxpr/psum | solution.py:9
  303.1 57.0 %all-reduce.6.cloned.1.call-start = ((), (), s32[]{:S(2)}) async-start(), calls=%async_computation.3 | async-start | bytes 262144 | tf_op jit(solution)/shard_map/while/body/eval_jaxpr/psum | solution.py:64
  305.0 92.5 %all-reduce.8.cloned.1.call-start = ((), (), s32[]{:S(2)}) async-start(), calls=%async_computation.4 | async-start | bytes 262144 | tf_op jit(solution)/shard_map/while/body/eval_jaxpr/psum | solution.py:9
  398.5 57.0 %all-reduce.6.cloned.1.call-start = ((), (), s32[]{:S(2)}) async-start(), calls=%async_computation.3 | async-start | bytes 262144 | tf_op jit(solution)/shard_map/while/body/eval_jaxpr/psum | solution.py:64
  400.4 92.5 %all-reduce.8.cloned.1.call-start = ((), (), s32[]{:S(2)}) async-start(), calls=%async_computation.4 | async-start | bytes 262144 | tf_op jit(solution)/shard_map/while/body/eval_jaxpr/psum | solution.py:9
  493.8 57.0 %all-reduce.6.cloned.1.call-start = ((), (), s32[]{:S(2)}) async-start(), calls=%async_computation.3 | async-start | bytes 262144 | tf_op jit(solution)/shard_map/while/body/eval_jaxpr/psum | solution.py:64
  495.7 92.5 %all-reduce.8.cloned.1.call-start = ((), (), s32[]{:S(2)}) async-start(), calls=%async_computation.4 | async-start | bytes 262144 | tf_op jit(solution)/shard_map/while/body/eval_jaxpr/psum | solution.py:9
  589.2 57.0 %all-reduce.6.cloned.1.call-start = ((), (), s32[]{:S(2)}) async-start(), calls=%async_computation.3 | async-start | bytes 262144 | tf_op jit(solution)/shard_map/while/body/eval_jaxpr/psum | solution.py:64
  591.1 92.5 %all-reduce.8.cloned.1.call-start = ((), (), s32[]{:S(2)}) async-start(), calls=%async_computation.4 | async-start | bytes 262144 | tf_op jit(solution)/shard_map/while/body/eval_jaxpr/psum | solution.py:9
  684.6 56.7 %all-reduce.6.cloned.1.call-start = ((), (), s32[]{:S(2)}) async-start(), calls=%async_computation.3 | async-start | bytes 262144 | tf_op jit(solution)/shard_map/while/body/eval_jaxpr/psum | solution.py:64
  686.4 92.2 %all-reduce.8.cloned.1.call-start = ((), (), s32[]{:S(2)}) async-start(), calls=%async_computation.4 | async-start | bytes 262144 | tf_op jit(solution)/shard_map/while/body/eval_jaxpr/psum | solution.py:9
  779.6 56.7 %all-reduce.6.cloned.1.call-start = ((), (), s32[]{:S(2)}) async-start(), calls=%async_computation.3 | async-start | bytes 262144 | tf_op jit(solution)/shard_map/while/body/eval_jaxpr/psum | solution.py:64
  781.5 92.2 %all-reduce.8.cloned.1.call-start = ((), (), s32[]{:S(2)}) async-start(), calls=%async_computation.4 | async-start | bytes 262144 | tf_op jit(solution)/shard_map/while/body/eval_jaxpr/psum | solution.py:9
  874.7 0.7 copy-start
Sparse Core Ops, SparseCore 0:
  27.5 29.9 reduce-scatter.1
  60.5 52.3 all-reduce.3
  116.8 52.8 all-reduce.5
  173.0 34.0 all-reduce.7
  211.6 53.1 all-reduce.5
  268.0 34.0 all-reduce.7
  307.0 53.1 all-reduce.5
  363.4 34.0 all-reduce.7
  402.3 53.1 all-reduce.5
  458.8 34.0 all-reduce.7
  497.7 53.1 all-reduce.5
  554.1 34.0 all-reduce.7
  593.0 53.1 all-reduce.5
  649.5 34.0 all-reduce.7
  688.1 53.1 all-reduce.5
  744.6 34.0 all-reduce.7
  783.2 53.1 all-reduce.5
  839.6 34.0 all-reduce.7
where the time goes:
time: 883 us; the launch traced here: 882 us
  waiting for transfers between devices  796 us (90%)
  matrix products  39.5 us (4%)
  local copies, waits for them, and re-layouts  28 us (3%)
  between operations  13.5 us (2%)
    psum x8, waiting for transfers between devices, advance(): summed = lax.psum(partial_value, 'col')  439 us
    psum x8, waiting for transfers between devices, broadcast(): return lax.psum(jnp.where(mine, shard, jnp.zeros_like(shard)), axis)  273 us
    psum x1, waiting for transfers between devices, per_device(): permuted = lax.psum(permuted, 'col')  53.7 us
    reduce_scatter x1, waiting for transfers between devices, per_device(): lax.psum_scatter(jnp.transpose(taken.reshape(rhs_count, blocks_here * lax...  30.1 us
    dot_general x8, matrix products, apply_inverse(): lax.dot_general(values, block_inv, (((1,), (1,)), ((), ())), precision=la...  25.1 us
  transfers between devices with their start and end apart: 18, of which 18 were waited for; matrix products, arithmetic and copies ran while one was open for 0% of the time, Pallas kernels for 0%

commit v1 on v0

--- a/solution.py
+++ b/solution.py
@@ -1,6 +1,10 @@
+import functools
+
 import jax
 import jax.numpy as jnp
 from jax import lax
+from jax.experimental import pallas as pl
+from jax.experimental.pallas import tpu as pltpu
 from jax.sharding import PartitionSpec as P
 
 
@@ -19,7 +23,7 @@
     )
 
 
-def per_device(rhs, pivots, factor, diag_inv):
+def per_device_general(rhs, pivots, factor, diag_inv):
     my_row = lax.axis_index("row")
     my_col = lax.axis_index("col")
     col_count = lax.axis_size("col")
@@ -77,6 +81,338 @@
     return lax.fori_loop(0, total_blocks, advance, start_state)
 
 
+MESH = pl.DeviceIdType.MESH
+HIGH = lax.Precision.HIGHEST
+
+
+def mul(a, b):
+    return jnp.dot(a, b, precision=HIGH, preferred_element_type=jnp.float32)
+
+
+def mul_t(a, b):
+    return lax.dot_general(
+        a, b, (((1,), (1,)), ((), ())), precision=HIGH, preferred_element_type=jnp.float32
+    )
+
+
+def solve_kernel(
+    rows,
+    cols,
+    g_ref,
+    fac_ref,
+    diag_ref,
+    out_ref,
+    lf,
+    dg,
+    s0,
+    a1,
+    b1,
+    ab2,
+    zbuf,
+    brow,
+    l10,
+    m,
+    w,
+    part,
+    pbuf,
+    ybuf,
+    local_sem,
+    ssend,
+    srecv,
+    zsend,
+    zrecv,
+    gsend,
+    grecv,
+    lsend,
+    lrecv,
+    psend,
+    precv,
+    ysend,
+    yrecv,
+):
+    r = lax.axis_index("row")
+    c = lax.axis_index("col")
+    core, x, y = c % 2, (c // 2) % 2, c // 4
+    half = rows // 2
+    blk = dg.shape[1]
+    plen = lf.shape[2]
+    slots = cols // 2
+    to_core = c + 1 - 2 * core
+    to_x = c + 2 * (1 - 2 * x)
+    to_y = c + 4 * (1 - 2 * y)
+
+    fetch = [
+        pltpu.make_async_copy(fac_ref.at[:, k, 0, :], lf.at[k], local_sem.at[k])
+        for k in range(rows)
+    ]
+    for copy in fetch:
+        copy.start()
+    fetch_d = pltpu.make_async_copy(diag_ref, dg, local_sem.at[rows])
+    fetch_d.start()
+
+    barrier = pltpu.get_barrier_semaphore()
+    for d in range(1, cols):
+        pl.semaphore_signal(barrier, inc=1, device_id=(r, (c + d) % cols), device_id_type=MESH)
+    for d in range(1, rows):
+        pl.semaphore_signal(barrier, inc=1, device_id=((r + d) % rows, c), device_id_type=MESH)
+    pl.semaphore_wait(barrier, cols + rows - 2)
+
+    def remote(src, dst, send, recv, row, col):
+        return pltpu.make_async_remote_copy(
+            src_ref=src,
+            dst_ref=dst,
+            send_sem=send,
+            recv_sem=recv,
+            device_id=(row, col),
+            device_id_type=MESH,
+        )
+
+    c0 = remote(g_ref.at[1 - core], s0, ssend.at[0], srecv.at[0], r, to_core)
+    c0.start()
+
+    mine = c % slots
+    xflip = mine + 2 * (1 - 2 * x)
+    cflip = mine + 1 - 2 * core
+    bflip = xflip + 1 - 2 * core
+    ly = remote(l10.at[mine], l10.at[mine], lsend.at[0], lrecv.at[0], r, to_y)
+    lx = remote(l10.at[mine], l10.at[mine], lsend.at[1], lrecv.at[1], r, to_x)
+    lc = remote(l10.at[mine], l10.at[mine], lsend.at[2], lrecv.at[2], r, to_core)
+    lb = remote(l10.at[xflip], l10.at[xflip], lsend.at[3], lrecv.at[3], r, to_core)
+    for copy in fetch:
+        copy.wait()
+
+    @pl.when(y == 0)
+    def _():
+        l10[mine] = lf[r, blk:, :]
+        ly.start()
+        lx.start()
+        lc.start()
+
+    c0.wait()
+    s0[...] += g_ref[core]
+    cxa = remote(s0.at[1 - x, :, pl.ds(0, half)], a1, ssend.at[1], srecv.at[1], r, to_x)
+    cyb = remote(s0.at[:, 1 - y, pl.ds(half, half)], b1, ssend.at[2], srecv.at[2], r, to_y)
+    cxa.start()
+    cyb.start()
+
+    @pl.when(y == 1)
+    def _():
+        ly.wait_recv()
+        lx.start()
+        lc.start()
+
+    cxa.wait()
+    a1[...] += s0[x, :, pl.ds(0, half)]
+    cya = remote(a1.at[1 - y], ab2.at[pl.ds(0, half)], ssend.at[3], srecv.at[3], r, to_y)
+    cya.start()
+    cyb.wait()
+    b1[...] += s0[:, y, pl.ds(half, half)]
+    cxb = remote(b1.at[1 - x], ab2.at[pl.ds(half, half)], ssend.at[4], srecv.at[4], r, to_x)
+    cxb.start()
+
+    fetch_d.wait()
+    lower = jnp.concatenate([lf[k, :blk, :] for k in range(rows - 1)], axis=1)
+    m[:blk, :] = mul(dg[0], lower)
+
+    cya.wait()
+    cxb.wait()
+    ab2[pl.ds(0, half)] += a1[y]
+    ab2[pl.ds(half, half)] += b1[x]
+    zc = [None]
+    for d in range(1, rows):
+        to = (r + d) % rows
+        copy = remote(ab2.at[to], zbuf.at[d], zsend.at[d], zrecv.at[d], to, c)
+        copy.start()
+        zc.append(copy)
+
+    lx.wait_recv()
+    lb.start()
+
+    for d in range(1, rows):
+        zc[d].wait_recv()
+    piece = ab2[r]
+    for d in range(1, rows):
+        piece = piece + zbuf[d]
+    brow[c] = piece
+    gc = [None]
+    for d in range(1, cols):
+        copy = remote(
+            brow.at[c], brow.at[c], gsend.at[d], grecv.at[d], r, (c + d) % cols
+        )
+        copy.start()
+        gc.append(copy)
+
+    lc.wait_recv()
+    lb.wait_recv()
+    l10v = jnp.concatenate([l10[t] for t in range(slots)], axis=1)
+    below = jnp.concatenate([lf[k, blk:, :] for k in range(rows - 1)], axis=1)
+    m[blk:, :] = mul(dg[1], below - mul(l10v, m[:blk, :]))
+
+    @pl.when(c < slots)
+    def _():
+        w[:, :blk] = dg[0, pl.ds(pl.multiple_of(mine * plen, plen), plen), :]
+        w[:, blk:] = jnp.zeros((plen, blk), jnp.float32)
+
+    @pl.when(c >= slots)
+    def _():
+        u = dg[1, pl.ds(pl.multiple_of(mine * plen, plen), plen), :]
+        w[:, blk:] = u
+        l10w = jnp.concatenate([l10[t] for t in range(slots)], axis=1)
+        w[:, :blk] = -mul(mul(u, l10w), dg[0])
+
+    for d in range(1, cols):
+        gc[d].wait_recv()
+    b = jnp.concatenate([brow[s] for s in range(cols)], axis=1)
+    own = mul_t(b, w[...])
+
+    pc = [
+        remote(
+            part.at[(c + d) % cols], pbuf.at[d], psend.at[d], precv.at[d], r, (c + d) % cols
+        )
+        for d in range(1, cols)
+    ]
+    for k in range(rows):
+        yc = [
+            remote(
+                ybuf.at[k],
+                ybuf.at[k],
+                ysend.at[d],
+                yrecv.at[k],
+                (k + d) % rows,
+                c,
+            )
+            for d in range(1, rows)
+        ]
+
+        @pl.when(r == k)
+        def _():
+            if k == 0:
+                ybuf[k] = own
+            else:
+                total = part[c]
+                for copy in pc:
+                    copy.wait_recv()
+                for d in range(1, cols):
+                    total = total + pbuf[d]
+                ybuf[k] = own - total
+            for copy in yc:
+                copy.start()
+
+        @pl.when(r != k)
+        def _():
+            yc[0].wait_recv()
+
+        if k < rows - 1:
+
+            @pl.when(r > k)
+            def _():
+                add = mul_t(ybuf[k], m[:, k * plen : (k + 1) * plen])
+                for p in range(cols):
+                    now = add[:, p * plen : (p + 1) * plen]
+                    part[p] = now if k == 0 else part[p] + now
+
+            @pl.when(r == k + 1)
+            def _():
+                for copy in pc:
+                    copy.start()
+
+    out_ref[...] = ybuf[...]
+
+    for d in range(1, rows):
+        zc[d].wait_send()
+
+    @pl.when(y == 0)
+    def _():
+        ly.wait_send()
+
+    lx.wait_send()
+    lc.wait_send()
+    lb.wait_send()
+    for d in range(1, cols):
+        gc[d].wait_send()
+
+    @pl.when(r > 0)
+    def _():
+        for copy in pc:
+            copy.wait_send()
+
+    for d in range(1, rows):
+        remote(
+            ybuf.at[r], ybuf.at[r], ysend.at[d], yrecv.at[r], (r + d) % rows, c
+        ).wait_send()
+
+
+def per_device_fast(rows, cols, rhs, pivots, factor, diag_inv):
+    my_row = lax.axis_index("row")
+    my_col = lax.axis_index("col")
+    nrhs, source_len = rhs.shape
+    plen = factor.shape[3]
+    blk = diag_inv.shape[1]
+    slab = factor.shape[0]
+    half = rows // 2
+    slots = cols // 2
+    first_column = (my_row * cols + my_col) * source_len
+    order = pivots.reshape(rows, 2, 2, 2, plen).transpose(3, 2, 1, 0, 4).reshape(-1)
+    located = order - first_column
+    inside = (located >= 0) & (located < source_len)
+    taken = jnp.take(rhs, jnp.clip(located, 0, source_len - 1), axis=1)
+    taken = jnp.where(inside[None, :], taken, 0.0)
+    g = taken.reshape(nrhs, 2, 2, 2, rows, plen).transpose(1, 2, 3, 4, 0, 5)
+    f32 = jnp.float32
+    dma = pltpu.SemaphoreType.DMA
+    solved = pl.pallas_call(
+        functools.partial(solve_kernel, rows, cols),
+        out_shape=jax.ShapeDtypeStruct((rows, nrhs, plen), f32),
+        in_specs=[
+            pl.BlockSpec(memory_space=pltpu.VMEM),
+            pl.BlockSpec(memory_space=pl.ANY),
+            pl.BlockSpec(memory_space=pl.ANY),
+        ],
+        out_specs=pl.BlockSpec(memory_space=pltpu.VMEM),
+        scratch_shapes=[
+            pltpu.VMEM((rows, slab, plen), f32),
+            pltpu.VMEM((2, blk, blk), f32),
+            pltpu.VMEM((2, 2, rows, nrhs, plen), f32),
+            pltpu.VMEM((2, half, nrhs, plen), f32),
+            pltpu.VMEM((2, half, nrhs, plen), f32),
+            pltpu.VMEM((rows, nrhs, plen), f32),
+            pltpu.VMEM((rows, nrhs, plen), f32),
+            pltpu.VMEM((cols, nrhs, plen), f32),
+            pltpu.VMEM((slots, blk, plen), f32),
+            pltpu.VMEM((slab, (rows - 1) * plen), f32),
+            pltpu.VMEM((plen, slab), f32),
+            pltpu.VMEM((cols, nrhs, plen), f32),
+            pltpu.VMEM((cols, nrhs, plen), f32),
+            pltpu.VMEM((rows, nrhs, plen), f32),
+            dma((rows + 1,)),
+            dma((5,)),
+            dma((5,)),
+            dma((rows,)),
+            dma((rows,)),
+            dma((cols,)),
+            dma((cols,)),
+            dma((4,)),
+            dma((4,)),
+            dma((cols,)),
+            dma((cols,)),
+            dma((rows,)),
+            dma((rows,)),
+        ],
+        compiler_params=pltpu.CompilerParams(collective_id=0, has_side_effects=True),
+    )(g, factor, diag_inv)
+    return jnp.transpose(solved, (1, 0, 2))[:, :, None, :]
+
+
+def per_device(rhs, pivots, factor, diag_inv):
+    rows = lax.axis_size("row")
+    cols = lax.axis_size("col")
+    slab, rounds, _, plen = factor.shape
+    blk = diag_inv.shape[1]
+    if cols == 8 and slab == 2 * blk == cols * plen and rounds == rows and rows % 2 == 0:
+        return per_device_fast(rows, cols, rhs, pivots, factor, diag_inv)
+    return per_device_general(rhs, pivots, factor, diag_inv)
+
+
 def solution(mesh):
     return jax.shard_map(
         per_device,

time: 883 us -> 82.8 us (0.09)
  waiting for transfers between devices: 796 us -> 0 us
  Pallas kernels: 0 us -> 59.8 us
  matrix products: 39.5 us -> 0 us
  between operations: 13.5 us -> 0.06 us
    psum x17 -> x0, waiting for transfers between devices: 766 us -> none  [the longest x8 439 us: advance(): summed = lax.psum(partial_value, 'col')]
    pallas_call x0 -> x1, Pallas kernels: none -> 59.8 us  [per_device_fast(): pl.pallas_call(functools.partial(solve_kernel, rows, cols), out_shape=jax...]
    dot_general x16 -> x0, matrix products: 39.5 us -> none  [the longest x8 25.1 us: apply_inverse(): lax.dot_general(values, block_inv, (((1,), (1,)), ((), ())), precision=la...]
    reduce_scatter x1 -> x0, waiting for transfers between devices: 30.1 us -> none  [per_device(): lax.psum_scatter(jnp.transpose(taken.reshape(rhs_count, blocks_here * lax...]
  transfers between devices with their start and end apart: 18 -> 0, of which waited for: 18 -> 0; matrix products, arithmetic and copies ran while one was open for 0% -> 0% of each run, Pallas kernels for 0% -> 0%
where the time goes in v1:
time: 82.8 us; the launch traced here: 82.4 us
  Pallas kernels  59.8 us (72%)
  local copies, waits for them, and re-layouts  19.8 us (24%)
  other arithmetic  2.72 us (3%)
    pallas_call x1, Pallas kernels, per_device_fast(): pl.pallas_call(functools.partial(solve_kernel, rows, cols), out_shape=jax...  59.8 us
    gather x2, local copies, waits for them, and re-layouts, per_device_fast(): taken = jnp.take(rhs, jnp.clip(located, 0, source_len - 1), axis=1)  16.3 us
    unnamed x1, local copies, waits for them, and re-layouts  1.82 us
    broadcast_in_dim x1, local copies, waits for them, and re-layouts, per_device_fast(): return jnp.transpose(solved, (1, 0, 2))[:, :, None, :]  1.69 us

profile of v1, /device:TPU:0, one launch (start us, length us, event | category | flops | bytes accessed | tf_op | source)
XLA Modules:
  0.0 82.4 jit_solution(17277999343860447537)
XLA Ops:
  0.0 0.7 compare_and_fusion.1
  0.8 0.7 subtract_clamp_fusion
  1.6 1.8 %copy.16 = f32[64,4096]{0,1:T(8,128)S(1)} copy(f32[64,4096]{1,0:T(8,128)} %param.4) | data formatting | bytes 2097152 | tf_op args[0]
  3.4 14.1 %gather_fusion = f32[4096,64]{1,0:T(8,128)} fusion(f32[64,4096]{0,1:T(8,128)S(1)} %copy.16, s32[4096]{0:T(1024)S(1)} %broadcast_clamp_fusion), kind=kCustom, calls=%fused_computation | custom fusion | bytes 2113536 | tf_op jit(solution)/shard_map/jit(_take)/gather | solution.py:358
  17.5 2.2 %copy.18 = f32[64,2,2,2,4,128]{5,0,4,3,2,1:T(8,128)S(1)} copy(f32[64,2,2,2,4,128]{0,5,4,3,2,1:T(8,128)} %bitcast.14) | data formatting | bytes 2097152 | tf_op jit(solution)/shard_map/jit(_take)/gather | solution.py:358
  19.7 1.2 %select_bitcast_fusion.g_ref = f32[2,2,2,4,64,128]{5,4,3,2,1,0:T(8,128)} fusion(f32[64,2,2,2,4,128]{5,0,4,3,2,1:T(8,128)S(1)} %copy.18, pred[2,2,2,4,128]{4,3,2,1,0:T(4,128)(4,1)S(1)} %copy.14, pred[2,2,2,4,128]{4,3,2,1,0:T(4,128)(4,1)S(1)} %copy.13), kind=kLoop, calls=%fused_computation.1 | loop fusion | flops 524288 | bytes 2105344 | tf_op jit(solution)/shard_map/transpose | solution.py:360
  20.9 59.8 %shard_map.46 = f32[4,64,128]{2,1,0:T(8,128)} custom-call(f32[2,2,2,4,64,128]{5,4,3,2,1,0:T(8,128)} %select_bitcast_fusion.g_ref, f32[1024,4,1,128]{3,2,1,0:T(1,128)} %fac_ref.1, f32[2,512,512]{2,1,0:T(8,128)} %diag_ref.1), custom_call_target="tpu_custom_call" | custom-call | tf_op jit(solution)/shard_map/pallas_call | solution.py:363
  80.7 1.7 %copy.19 = f32[64,4,1,128]{3,2,1,0:T(1,128)} copy(f32[64,4,1,128]{3,0,1,2:T(8,128)} %bitcast.15) | data formatting | bytes 262144 | tf_op jit(solution)/shard_map/broadcast_in_dim | solution.py:403
  (7 shorter events, 0.1 us)

commit v2 on v1

--- a/solution.py
+++ b/solution.py
@@ -82,36 +82,42 @@
 
 
 MESH = pl.DeviceIdType.MESH
-HIGH = lax.Precision.HIGHEST
-
-
-def mul(a, b):
-    return jnp.dot(a, b, precision=HIGH, preferred_element_type=jnp.float32)
-
-
-def mul_t(a, b):
-    return lax.dot_general(
-        a, b, (((1,), (1,)), ((), ())), precision=HIGH, preferred_element_type=jnp.float32
+def split(a):
+    hi = a.astype(jnp.bfloat16)
+    return hi, (a - hi.astype(jnp.float32)).astype(jnp.bfloat16)
+
+
+def dot3(a, b, transposed=False):
+    dims = (((1,), (1 if transposed else 0,)), ((), ()))
+    one = functools.partial(
+        lax.dot_general, dimension_numbers=dims, preferred_element_type=jnp.float32
     )
+    return one(a[0], b[0]) + (one(a[0], b[1]) + one(a[1], b[0]))
 
 
 def solve_kernel(
     rows,
     cols,
-    g_ref,
+    rhs_ref,
+    piv_ref,
     fac_ref,
     diag_ref,
     out_ref,
     lf,
     dg,
+    dh,
+    dl,
+    g,
     s0,
     a1,
-    b1,
-    ab2,
+    ab,
     zbuf,
     brow,
     l10,
-    m,
+    lh,
+    ll,
+    mh,
+    ml,
     w,
     part,
     pbuf,
@@ -133,7 +139,7 @@
     r = lax.axis_index("row")
     c = lax.axis_index("col")
     core, x, y = c % 2, (c // 2) % 2, c // 4
-    half = rows // 2
+    nrhs, source_len = rhs_ref.shape
     blk = dg.shape[1]
     plen = lf.shape[2]
     slots = cols // 2
@@ -155,7 +161,6 @@
         pl.semaphore_signal(barrier, inc=1, device_id=(r, (c + d) % cols), device_id_type=MESH)
     for d in range(1, rows):
         pl.semaphore_signal(barrier, inc=1, device_id=((r + d) % rows, c), device_id_type=MESH)
-    pl.semaphore_wait(barrier, cols + rows - 2)
 
     def remote(src, dst, send, recv, row, col):
         return pltpu.make_async_remote_copy(
@@ -167,103 +172,174 @@
             device_id_type=MESH,
         )
 
-    c0 = remote(g_ref.at[1 - core], s0, ssend.at[0], srecv.at[0], r, to_core)
-    c0.start()
+    first_tile = (r * cols + c) * (source_len // plen)
+
+    def pick(p, side):
+        @pl.loop(0, 4)
+        def _(i):
+            f, s = i // 2, i % 2
+            q = (s * 4 + f * 2 if p % 2 == 0 else f * 4 + s * 2) + side + p * cols
+            wanted = jnp.broadcast_to(piv_ref[q], (8, plen))
+            lane = wanted % plen
+            tile = wanted // plen - first_tile
+            for n in range(nrhs // 8):
+                found = jnp.zeros((8, plen), jnp.float32)
+                for t in range(source_len // plen):
+                    got = jnp.take_along_axis(
+                        rhs_ref[n * 8 : n * 8 + 8, t * plen : (t + 1) * plen],
+                        lane,
+                        axis=1,
+                        mode="promise_in_bounds",
+                    )
+                    found = jnp.where(tile == t, got, found)
+                g[p, side, f, s, n * 8 : n * 8 + 8, :] = found
 
     mine = c % slots
     xflip = mine + 2 * (1 - 2 * x)
-    cflip = mine + 1 - 2 * core
-    bflip = xflip + 1 - 2 * core
     ly = remote(l10.at[mine], l10.at[mine], lsend.at[0], lrecv.at[0], r, to_y)
     lx = remote(l10.at[mine], l10.at[mine], lsend.at[1], lrecv.at[1], r, to_x)
     lc = remote(l10.at[mine], l10.at[mine], lsend.at[2], lrecv.at[2], r, to_core)
     lb = remote(l10.at[xflip], l10.at[xflip], lsend.at[3], lrecv.at[3], r, to_core)
-    for copy in fetch:
-        copy.wait()
-
-    @pl.when(y == 0)
-    def _():
-        l10[mine] = lf[r, blk:, :]
-        ly.start()
-        lx.start()
-        lc.start()
-
-    c0.wait()
-    s0[...] += g_ref[core]
-    cxa = remote(s0.at[1 - x, :, pl.ds(0, half)], a1, ssend.at[1], srecv.at[1], r, to_x)
-    cyb = remote(s0.at[:, 1 - y, pl.ds(half, half)], b1, ssend.at[2], srecv.at[2], r, to_y)
-    cxa.start()
-    cyb.start()
-
-    @pl.when(y == 1)
-    def _():
-        ly.wait_recv()
-        lx.start()
-        lc.start()
-
-    cxa.wait()
-    a1[...] += s0[x, :, pl.ds(0, half)]
-    cya = remote(a1.at[1 - y], ab2.at[pl.ds(0, half)], ssend.at[3], srecv.at[3], r, to_y)
-    cya.start()
-    cyb.wait()
-    b1[...] += s0[:, y, pl.ds(half, half)]
-    cxb = remote(b1.at[1 - x], ab2.at[pl.ds(half, half)], ssend.at[4], srecv.at[4], r, to_x)
-    cxb.start()
+
+    c0, c1, c2, cz = [], [], [], []
+    for p in range(rows):
+        near, far = ((x, to_x), (y, to_y)) if p % 2 == 0 else ((y, to_y), (x, to_x))
+        c0.append(
+            remote(g.at[p, 1 - core], s0.at[p], ssend.at[p], srecv.at[p], r, to_core)
+        )
+        c1.append(
+            remote(
+                s0.at[p, 1 - near[0]],
+                a1.at[p],
+                ssend.at[rows + p],
+                srecv.at[rows + p],
+                r,
+                near[1],
+            )
+        )
+        c2.append(
+            remote(
+                a1.at[p, 1 - far[0]],
+                ab.at[p],
+                ssend.at[2 * rows + p],
+                srecv.at[2 * rows + p],
+                r,
+                far[1],
+            )
+        )
+        hop = (p - r + rows) % rows
+        cz.append(remote(ab.at[p], zbuf.at[hop], zsend.at[p], zrecv.at[hop], p, c))
+    gc = [
+        remote(brow.at[c], brow.at[c], gsend.at[d], grecv.at[d], r, (c + d) % cols)
+        for d in range(1, cols)
+    ]
+
+    def landed_core(p):
+        c0[p].wait()
+        s0[p] += g[p, core]
+        c1[p].start()
+
+    def landed_near(p):
+        near, far = (x, y) if p % 2 == 0 else (y, x)
+        c1[p].wait()
+        a1[p] += s0[p, near]
+        c2[p].start()
+
+    def landed_far(p):
+        far = y if p % 2 == 0 else x
+        c2[p].wait()
+        ab[p] += a1[p, far]
+
+        @pl.when(r != p)
+        def _():
+            cz[p].start()
+
+    def landed_row(p):
+        @pl.when(r == p)
+        def _():
+            piece = ab[p]
+            for d in range(1, rows):
+                remote(
+                    ab.at[p], zbuf.at[d], zsend.at[p], zrecv.at[d], (p + d) % rows, c
+                ).wait_recv()
+                piece = piece + zbuf[d]
+            brow[c] = piece
+            for copy in gc:
+                copy.start()
+
+    for step in range(rows + 4):
+        if step < rows:
+            pick(step, 1 - core)
+            if step == 0:
+                pl.semaphore_wait(barrier, cols + rows - 2)
+            c0[step].start()
+            pick(step, core)
+        if step == 0:
+            for copy in fetch:
+                copy.wait()
+
+            @pl.when(y == 0)
+            def _():
+                l10[mine] = lf[r, blk:, :]
+                ly.start()
+
+        for stage, act in ((4, landed_row), (3, landed_far), (2, landed_near), (1, landed_core)):
+            if 0 <= step - stage < rows:
+                act(step - stage)
+        if step == 3:
+
+            @pl.when(y == 1)
+            def _():
+                ly.wait_recv()
+
+            lx.start()
+            lc.start()
 
     fetch_d.wait()
-    lower = jnp.concatenate([lf[k, :blk, :] for k in range(rows - 1)], axis=1)
-    m[:blk, :] = mul(dg[0], lower)
-
-    cya.wait()
-    cxb.wait()
-    ab2[pl.ds(0, half)] += a1[y]
-    ab2[pl.ds(half, half)] += b1[x]
-    zc = [None]
-    for d in range(1, rows):
-        to = (r + d) % rows
-        copy = remote(ab2.at[to], zbuf.at[d], zsend.at[d], zrecv.at[d], to, c)
-        copy.start()
-        zc.append(copy)
+    for i in range(2):
+        dh[i], dl[i] = split(dg[i])
+
+    def top(k, carry):
+        th, tl = split(dot3((dh[0], dl[0]), split(lf[k, :blk, :])))
+        mh[k, :blk, :] = th
+        ml[k, :blk, :] = tl
+        return carry
+
+    lax.fori_loop(0, r, top, 0)
 
     lx.wait_recv()
     lb.start()
-
-    for d in range(1, rows):
-        zc[d].wait_recv()
-    piece = ab2[r]
-    for d in range(1, rows):
-        piece = piece + zbuf[d]
-    brow[c] = piece
-    gc = [None]
-    for d in range(1, cols):
-        copy = remote(
-            brow.at[c], brow.at[c], gsend.at[d], grecv.at[d], r, (c + d) % cols
-        )
-        copy.start()
-        gc.append(copy)
-
     lc.wait_recv()
     lb.wait_recv()
-    l10v = jnp.concatenate([l10[t] for t in range(slots)], axis=1)
-    below = jnp.concatenate([lf[k, blk:, :] for k in range(rows - 1)], axis=1)
-    m[blk:, :] = mul(dg[1], below - mul(l10v, m[:blk, :]))
+    for t in range(slots):
+        lh[:, t * plen : (t + 1) * plen], ll[:, t * plen : (t + 1) * plen] = split(l10[t])
+
+    rows_here = pl.ds(pl.multiple_of(mine * plen, plen), plen)
 
     @pl.when(c < slots)
     def _():
-        w[:, :blk] = dg[0, pl.ds(pl.multiple_of(mine * plen, plen), plen), :]
+        w[:, :blk] = dg[0, rows_here, :]
         w[:, blk:] = jnp.zeros((plen, blk), jnp.float32)
 
     @pl.when(c >= slots)
     def _():
-        u = dg[1, pl.ds(pl.multiple_of(mine * plen, plen), plen), :]
-        w[:, blk:] = u
-        l10w = jnp.concatenate([l10[t] for t in range(slots)], axis=1)
-        w[:, :blk] = -mul(mul(u, l10w), dg[0])
-
-    for d in range(1, cols):
-        gc[d].wait_recv()
+        w[:, blk:] = dg[1, rows_here, :]
+        u = dot3((dh[1, rows_here, :], dl[1, rows_here, :]), (lh[...], ll[...]))
+        w[:, :blk] = -dot3(split(u), (dh[0], dl[0]))
+
+    def bottom(k, carry):
+        low = lf[k, blk:, :] - dot3((lh[...], ll[...]), (mh[k, :blk, :], ml[k, :blk, :]))
+        bh, bl = split(dot3((dh[1], dl[1]), split(low)))
+        mh[k, blk:, :] = bh
+        ml[k, blk:, :] = bl
+        return carry
+
+    lax.fori_loop(0, r, bottom, 0)
+
+    for copy in gc:
+        copy.wait_recv()
     b = jnp.concatenate([brow[s] for s in range(cols)], axis=1)
-    own = mul_t(b, w[...])
+    own = dot3(split(b), split(w[...]), True)
 
     pc = [
         remote(
@@ -273,14 +349,7 @@
     ]
     for k in range(rows):
         yc = [
-            remote(
-                ybuf.at[k],
-                ybuf.at[k],
-                ysend.at[d],
-                yrecv.at[k],
-                (k + d) % rows,
-                c,
-            )
+            remote(ybuf.at[k], ybuf.at[k], ysend.at[d], yrecv.at[k], (k + d) % rows, c)
             for d in range(1, rows)
         ]
 
@@ -290,9 +359,8 @@
                 ybuf[k] = own
             else:
                 total = part[c]
-                for copy in pc:
-                    copy.wait_recv()
                 for d in range(1, cols):
+                    pc[d - 1].wait_recv()
                     total = total + pbuf[d]
                 ybuf[k] = own - total
             for copy in yc:
@@ -306,7 +374,7 @@
 
             @pl.when(r > k)
             def _():
-                add = mul_t(ybuf[k], m[:, k * plen : (k + 1) * plen])
+                add = dot3(split(ybuf[k]), (mh[k], ml[k]), True)
                 for p in range(cols):
                     now = add[:, p * plen : (p + 1) * plen]
                     part[p] = now if k == 0 else part[p] + now
@@ -318,8 +386,11 @@
 
     out_ref[...] = ybuf[...]
 
-    for d in range(1, rows):
-        zc[d].wait_send()
+    for p in range(rows):
+
+        @pl.when(r != p)
+        def _():
+            cz[p].wait_send()
 
     @pl.when(y == 0)
     def _():
@@ -328,8 +399,8 @@
     lx.wait_send()
     lc.wait_send()
     lb.wait_send()
-    for d in range(1, cols):
-        gc[d].wait_send()
+    for copy in gc:
+        copy.wait_send()
 
     @pl.when(r > 0)
     def _():
@@ -343,27 +414,18 @@
 
 
 def per_device_fast(rows, cols, rhs, pivots, factor, diag_inv):
-    my_row = lax.axis_index("row")
-    my_col = lax.axis_index("col")
-    nrhs, source_len = rhs.shape
+    nrhs = rhs.shape[0]
     plen = factor.shape[3]
     blk = diag_inv.shape[1]
     slab = factor.shape[0]
-    half = rows // 2
     slots = cols // 2
-    first_column = (my_row * cols + my_col) * source_len
-    order = pivots.reshape(rows, 2, 2, 2, plen).transpose(3, 2, 1, 0, 4).reshape(-1)
-    located = order - first_column
-    inside = (located >= 0) & (located < source_len)
-    taken = jnp.take(rhs, jnp.clip(located, 0, source_len - 1), axis=1)
-    taken = jnp.where(inside[None, :], taken, 0.0)
-    g = taken.reshape(nrhs, 2, 2, 2, rows, plen).transpose(1, 2, 3, 4, 0, 5)
-    f32 = jnp.float32
+    f32, bf16 = jnp.float32, jnp.bfloat16
     dma = pltpu.SemaphoreType.DMA
     solved = pl.pallas_call(
         functools.partial(solve_kernel, rows, cols),
         out_shape=jax.ShapeDtypeStruct((rows, nrhs, plen), f32),
         in_specs=[
+            pl.BlockSpec(memory_space=pltpu.VMEM),
             pl.BlockSpec(memory_space=pltpu.VMEM),
             pl.BlockSpec(memory_space=pl.ANY),
             pl.BlockSpec(memory_space=pl.ANY),
@@ -372,21 +434,26 @@
         scratch_shapes=[
             pltpu.VMEM((rows, slab, plen), f32),
             pltpu.VMEM((2, blk, blk), f32),
-            pltpu.VMEM((2, 2, rows, nrhs, plen), f32),
-            pltpu.VMEM((2, half, nrhs, plen), f32),
-            pltpu.VMEM((2, half, nrhs, plen), f32),
+            pltpu.VMEM((2, blk, blk), bf16),
+            pltpu.VMEM((2, blk, blk), bf16),
+            pltpu.VMEM((rows, 2, 2, 2, nrhs, plen), f32),
+            pltpu.VMEM((rows, 2, 2, nrhs, plen), f32),
+            pltpu.VMEM((rows, 2, nrhs, plen), f32),
             pltpu.VMEM((rows, nrhs, plen), f32),
             pltpu.VMEM((rows, nrhs, plen), f32),
             pltpu.VMEM((cols, nrhs, plen), f32),
             pltpu.VMEM((slots, blk, plen), f32),
-            pltpu.VMEM((slab, (rows - 1) * plen), f32),
+            pltpu.VMEM((blk, blk), bf16),
+            pltpu.VMEM((blk, blk), bf16),
+            pltpu.VMEM((rows - 1, slab, plen), bf16),
+            pltpu.VMEM((rows - 1, slab, plen), bf16),
             pltpu.VMEM((plen, slab), f32),
             pltpu.VMEM((cols, nrhs, plen), f32),
             pltpu.VMEM((cols, nrhs, plen), f32),
             pltpu.VMEM((rows, nrhs, plen), f32),
             dma((rows + 1,)),
-            dma((5,)),
-            dma((5,)),
+            dma((3 * rows,)),
+            dma((3 * rows,)),
             dma((rows,)),
             dma((rows,)),
             dma((cols,)),
@@ -399,7 +466,7 @@
             dma((rows,)),
         ],
         compiler_params=pltpu.CompilerParams(collective_id=0, has_side_effects=True),
-    )(g, factor, diag_inv)
+    )(rhs, pivots.reshape(rows * cols, 1, plen), factor, diag_inv)
     return jnp.transpose(solved, (1, 0, 2))[:, :, None, :]
 
 
@@ -408,7 +475,7 @@
     cols = lax.axis_size("col")
     slab, rounds, _, plen = factor.shape
     blk = diag_inv.shape[1]
-    if cols == 8 and slab == 2 * blk == cols * plen and rounds == rows and rows % 2 == 0:
+    if cols == 8 and slab == 2 * blk == cols * plen and rounds == rows and rhs.shape[1] % plen == 0:
         return per_device_fast(rows, cols, rhs, pivots, factor, diag_inv)
     return per_device_general(rhs, pivots, factor, diag_inv)
 

time: 82.8 us -> 62 us (0.75)
  local copies, waits for them, and re-layouts: 19.8 us -> 1.69 us
  other arithmetic: 2.72 us -> 0 us
    gather x2 -> x0, local copies, waits for them, and re-layouts: 16.3 us -> none  [per_device_fast(): taken = jnp.take(rhs, jnp.clip(located, 0, source_len - 1), axis=1)]
    unnamed x1 -> x0, local copies, waits for them, and re-layouts: 1.82 us -> none
    transpose x1 -> x0, other arithmetic: 1.22 us -> none  [per_device_fast(): g = taken.reshape(nrhs, 2, 2, 2, rows, plen).transpose(1, 2, 3, 4, 0, 5)]
where the time goes in v2:
time: 62 us; the launch traced here: 61.8 us
  Pallas kernels  60.1 us (97%)
  local copies, waits for them, and re-layouts  1.69 us (3%)
    pallas_call x1, Pallas kernels, per_device_fast(): pl.pallas_call(functools.partial(solve_kernel, rows, cols), out_shape=jax...  60.1 us
    broadcast_in_dim x1, local copies, waits for them, and re-layouts, per_device_fast(): return jnp.transpose(solved, (1, 0, 2))[:, :, None, :]  1.69 us

profile of v2, /device:TPU:0, one launch (start us, length us, event | category | flops | bytes accessed | tf_op | source)
XLA Modules:
  0.0 61.8 jit_solution(14382726879217110773)
XLA Ops:
  0.0 60.1 %shard_map.46 = f32[4,64,128]{2,1,0:T(8,128)} custom-call(f32[64,4096]{1,0:T(8,128)} %rhs_ref.1, s32[32,1,128]{2,1,0:T(1,128)} %bitcast.5, f32[1024,4,1,128]{3,2,1,0:T(1,128)} %fac_ref.1, f32[2,512,512]{2,1,0:T(8,128)} %diag_ref.1), custom_call_target="tpu_custom_call" | custom-call | tf_op jit(solution)/shard_map/pallas_call | solution.py:424
  60.1 1.7 %copy.5 = f32[64,4,1,128]{3,2,1,0:T(1,128)} copy(f32[64,4,1,128]{3,0,1,2:T(8,128)} %bitcast.4) | data formatting | bytes 262144 | tf_op jit(solution)/shard_map/broadcast_in_dim | solution.py:470

commit v3 on v2

--- a/solution.py
+++ b/solution.py
@@ -341,50 +341,90 @@
     b = jnp.concatenate([brow[s] for s in range(cols)], axis=1)
     own = dot3(split(b), split(w[...]), True)
 
-    pc = [
-        remote(
-            part.at[(c + d) % cols], pbuf.at[d], psend.at[d], precv.at[d], r, (c + d) % cols
-        )
-        for d in range(1, cols)
-    ]
-    for k in range(rows):
-        yc = [
-            remote(ybuf.at[k], ybuf.at[k], ysend.at[d], yrecv.at[k], (k + d) % rows, c)
+    def pieces_of(h):
+        return [
+            remote(
+                part.at[h, (c + d) % cols],
+                pbuf.at[h, d],
+                psend.at[h, d],
+                precv.at[h, d],
+                r,
+                (c + d) % cols,
+            )
+            for d in range(1, cols)
+        ]
+
+    def news_of(k, h):
+        return [
+            remote(
+                ybuf.at[k, h],
+                ybuf.at[k, h],
+                ysend.at[h, d],
+                yrecv.at[h, k],
+                (k + d) % rows,
+                c,
+            )
             for d in range(1, rows)
         ]
 
-        @pl.when(r == k)
-        def _():
-            if k == 0:
-                ybuf[k] = own
-            else:
-                total = part[c]
-                for d in range(1, cols):
-                    pc[d - 1].wait_recv()
-                    total = total + pbuf[d]
-                ybuf[k] = own - total
-            for copy in yc:
-                copy.start()
-
-        @pl.when(r != k)
-        def _():
-            yc[0].wait_recv()
-
-        if k < rows - 1:
-
-            @pl.when(r > k)
+    chains = ybuf.shape[1]
+    group = nrhs // chains
+    for k in range(rows):
+        for h in range(chains):
+            pc = pieces_of(h)
+            yc = news_of(k, h)
+            own_h = own[h * group : (h + 1) * group]
+
+            @pl.when(r == k)
             def _():
-                add = dot3(split(ybuf[k]), (mh[k], ml[k]), True)
-                for p in range(cols):
-                    now = add[:, p * plen : (p + 1) * plen]
-                    part[p] = now if k == 0 else part[p] + now
-
-            @pl.when(r == k + 1)
+                if k == 0:
+                    ybuf[k, h] = own_h
+                else:
+                    total = part[h, c]
+                    for d in range(1, cols):
+                        pc[d - 1].wait_recv()
+                        total = total + pbuf[h, d]
+                    ybuf[k, h] = own_h - total
+                for copy in yc:
+                    copy.start()
+
+            @pl.when(r != k)
             def _():
-                for copy in pc:
-                    copy.start()
-
-    out_ref[...] = ybuf[...]
+                yc[0].wait_recv()
+
+            if k < rows - 1:
+
+                @pl.when(r > k)
+                def _():
+                    add = dot3(split(ybuf[k, h]), (mh[k], ml[k]), True)
+                    for p in range(cols):
+                        now = add[:, p * plen : (p + 1) * plen]
+                        part[h, p] = now if k == 0 else part[h, p] + now
+
+                @pl.when(r == k + 1)
+                def _():
+                    for copy in pc:
+                        copy.start()
+
+    for h in range(chains):
+        out_ref[:, h * group : (h + 1) * group, :] = ybuf[:, h]
+
+    @pl.when(r > 0)
+    def _():
+        for h in range(chains):
+            for copy in pieces_of(h):
+                copy.wait_send()
+
+    for h in range(chains):
+        for d in range(1, rows):
+            remote(
+                ybuf.at[r, h],
+                ybuf.at[r, h],
+                ysend.at[h, d],
+                yrecv.at[h, r],
+                (r + d) % rows,
+                c,
+            ).wait_send()
 
     for p in range(rows):
 
@@ -401,16 +441,6 @@
     lb.wait_send()
     for copy in gc:
         copy.wait_send()
-
-    @pl.when(r > 0)
-    def _():
-        for copy in pc:
-            copy.wait_send()
-
-    for d in range(1, rows):
-        remote(
-            ybuf.at[r], ybuf.at[r], ysend.at[d], yrecv.at[r], (r + d) % rows, c
-        ).wait_send()
 
 
 def per_device_fast(rows, cols, rhs, pivots, factor, diag_inv):
@@ -419,6 +449,7 @@
     blk = diag_inv.shape[1]
     slab = factor.shape[0]
     slots = cols // 2
+    chains = 2 if nrhs % 16 == 0 else 1
     f32, bf16 = jnp.float32, jnp.bfloat16
     dma = pltpu.SemaphoreType.DMA
     solved = pl.pallas_call(
@@ -448,9 +479,9 @@
             pltpu.VMEM((rows - 1, slab, plen), bf16),
             pltpu.VMEM((rows - 1, slab, plen), bf16),
             pltpu.VMEM((plen, slab), f32),
-            pltpu.VMEM((cols, nrhs, plen), f32),
-            pltpu.VMEM((cols, nrhs, plen), f32),
-            pltpu.VMEM((rows, nrhs, plen), f32),
+            pltpu.VMEM((chains, cols, nrhs // chains, plen), f32),
+            pltpu.VMEM((chains, cols, nrhs // chains, plen), f32),
+            pltpu.VMEM((rows, chains, nrhs // chains, plen), f32),
             dma((rows + 1,)),
             dma((3 * rows,)),
             dma((3 * rows,)),
@@ -460,10 +491,10 @@
             dma((cols,)),
             dma((4,)),
             dma((4,)),
-            dma((cols,)),
-            dma((cols,)),
-            dma((rows,)),
-            dma((rows,)),
+            dma((chains, cols)),
+            dma((chains, cols)),
+            dma((chains, rows)),
+            dma((chains, rows)),
         ],
         compiler_params=pltpu.CompilerParams(collective_id=0, has_side_effects=True),
     )(rhs, pivots.reshape(rows * cols, 1, plen), factor, diag_inv)

time: 62 us -> 60.4 us (0.974)
  Pallas kernels: 60.1 us -> 58.6 us
    pallas_call x1, Pallas kernels: 60.1 us -> 58.6 us  [per_device_fast(): pl.pallas_call(functools.partial(solve_kernel, rows, cols), out_shape=jax...]
where the time goes in v3:
time: 60.4 us; the launch traced here: 60.3 us
  Pallas kernels  58.6 us (97%)
  local copies, waits for them, and re-layouts  1.69 us (3%)
    pallas_call x1, Pallas kernels, per_device_fast(): pl.pallas_call(functools.partial(solve_kernel, rows, cols), out_shape=jax...  58.6 us
    broadcast_in_dim x1, local copies, waits for them, and re-layouts, per_device_fast(): return jnp.transpose(solved, (1, 0, 2))[:, :, None, :]  1.69 us

profile of v3, /device:TPU:0, one launch (start us, length us, event | category | flops | bytes accessed | tf_op | source)
XLA Modules:
  0.0 60.3 jit_solution(10940148648639198380)
XLA Ops:
  0.0 58.6 %shard_map.46 = f32[4,64,128]{2,1,0:T(8,128)} custom-call(f32[64,4096]{1,0:T(8,128)} %rhs_ref.1, s32[32,1,128]{2,1,0:T(1,128)} %bitcast.5, f32[1024,4,1,128]{3,2,1,0:T(1,128)} %fac_ref.1, f32[2,512,512]{2,1,0:T(8,128)} %diag_ref.1), custom_call_target="tpu_custom_call" | custom-call | tf_op jit(solution)/shard_map/pallas_call | solution.py:455
  58.6 1.7 %copy.5 = f32[64,4,1,128]{3,2,1,0:T(1,128)} copy(f32[64,4,1,128]{3,0,1,2:T(8,128)} %bitcast.4) | data formatting | bytes 262144 | tf_op jit(solution)/shard_map/broadcast_in_dim | solution.py:501
